TPU v7x, 32 devices: a whole 2x2x4 slice. The times are simulated.
32 devices in a mesh: dev: 8 (over z, x), rep: 4 (over y, core).
Axes of the slice: x: 2, y: 2, z: 4, core: 2. Of those that a mesh axis runs over, the one named last changes fastest.
Arguments:
- h_zero: bfloat16 [32768, 256], P(('dev', 'rep')), may hold values from 0 to 2
- h_prev: bfloat16 [32768, 256], P(('dev', 'rep')), may hold values from 0 to 2
- hist_a: bfloat16 [32768, 256], P('dev'), may hold values from 0 to 2
- hist_b: bfloat16 [32768, 256], P('dev'), may hold values from 0 to 2
- tile_vals: bfloat16 [256, 12, 128, 128], P(('dev', 'rep'))
- tile_cols: int32 [256, 12], P(('dev', 'rep')), may hold values from 0 to 47, as said below
- pull_rows: int32 [32, 8, 128], P(('dev', 'rep')), may hold values from 0 to 4095
- pull_counts: int32 [32, 8], P(('dev', 'rep')), may hold values from 96 to 128, as said below
- weight_two: bfloat16 [256, 256], replicated, may hold values from -0.375 to 0.375
- weight_three: bfloat16 [256, 256], replicated, may hold values from -0.375 to 0.375
- grad_out: bfloat16 [32768, 256], P(('dev', 'rep')), may hold values from -0.125 to 0.125
Outputs:
- layer_three: bfloat16 [32768, 256], P(('dev', 'rep'))
- new_history: bfloat16 [32768, 256], P('dev')
- weight_grad: float32 [256, 256], replicated
Inputs may be any that keep to these rules, and one draw needn't show every extreme that they name: `tile_cols`: entry 0 of a row block names one of its device's own 8 blocks; entries 1 to 3 name blocks of the owner's history shard; the other 8 name pulled blocks of consecutive owners modulo 8, and every owner's block is named by some row block of each device. `pull_rows`: entries at slots at or past the block's count are read by no output. `pull_counts`: every device pulls a full block of 128 rows from some owner and a block of exactly 96 rows from another.
All inputs are finite; a program needn't handle non-finite values.
Results may differ from a plain program's by a relative error of at most 0.0034.
Values may be sent and summed in bfloat16 or wider, within the bound.
A program may use at most 128 MiB of HBM per device.

v0:
```python
import functools
import math

import jax
import jax.numpy as jnp
from jax import lax
from jax.experimental import pallas as pl
from jax.experimental.pallas import tpu as pltpu
from jax.sharding import PartitionSpec as P

restart = 0.1
strength = 0.5
MESH = pl.DeviceIdType.MESH


def kernel(
    D, R,
    cols, counts, rows_in,
    h_zero, h_prev, hist_a, hist_b, tile_vals, w_two, w_three, grad_out,
    layer_out, hist_out, grad_res,
    zero_v, cur_v, hist_av, hist_bv, vals_v, w2_v, w3_v, up_v,
    ask, asked, col, send_a, send_b, pull_a, pull_b, acc, acc_a, acc_b,
    fresh_v, low_v, g_send, g_mate, g_recv, g_part, g_all,
    local_sem, idx_s, idx_r, a_s, a_r, b_s, b_r, f_s, f_r, m_s, m_r, g_s, g_r, p_s, p_r,
):
    N = D * R
    d = lax.axis_index("dev")
    r = lax.axis_index("rep")
    me = d * R + r
    slots = rows_in.shape[2]
    feat = hist_av.shape[2]
    blocks = vals_v.shape[0]
    tiles = vals_v.shape[1]
    home = 4
    home_blocks = hist_av.shape[0]

    loads = [
        (hist_a, hist_av), (tile_vals, vals_v), (h_prev, cur_v), (hist_b, hist_bv),
        (h_zero, zero_v), (w_two, w2_v), (w_three, w3_v), (grad_out, up_v),
    ]
    copies = [pltpu.make_async_copy(s, t, local_sem.at[i]) for i, (s, t) in enumerate(loads)]
    for c in copies:
        c.start()

    barrier = pltpu.get_barrier_semaphore()

    def greet(k, _):
        t = lax.rem(me + 1 + k, N)
        pl.semaphore_signal(
            barrier, inc=1, device_id=(lax.div(t, R), lax.rem(t, R)), device_id_type=MESH
        )
        return 0

    lax.fori_loop(0, N - 1, greet, 0)

    lane = lax.broadcasted_iota(jnp.int32, (1, slots), 1)

    def mask_rows(p, _):
        ask[p] = jnp.where(lane < counts[0, p], rows_in[0, pl.ds(p, 1), :], -1)
        return 0

    lax.fori_loop(0, D, mask_rows, 0)
    pl.semaphore_wait(barrier, N - 1)

    def offset(j):
        return D // 2 + lax.div(j + 1, 2) * (1 - 2 * lax.rem(j, 2))

    def send_rows(j, _):
        p = lax.rem(d + offset(j), D)
        pltpu.make_async_remote_copy(
            src_ref=ask.at[p], dst_ref=asked.at[d], send_sem=idx_s, recv_sem=idx_r,
            device_id=(p, r), device_id_type=MESH,
        ).start()
        return 0

    lax.fori_loop(0, D - 1, send_rows, 0)
    asked[d] = ask[d]

    def whole(ref, n, s, q):
        part = ref.at[pl.ds(0, n)]
        return pltpu.make_async_remote_copy(
            src_ref=part, dst_ref=part, send_sem=s, recv_sem=q,
            device_id=(lax.rem(d + 1, D), r), device_id_type=MESH,
        )

    whole(asked, D - 1, idx_s, idx_r).wait_recv()

    def column(j, _):
        q = lax.rem(d + D - offset(j), D)
        col[j] = jnp.broadcast_to(asked[q], (slots, slots)).T
        return 0

    lax.fori_loop(0, D, column, 0)

    group = 2 if D % 2 == 0 else 1
    chunk_blocks = 8
    depth = chunk_blocks * slots
    lanes = lax.broadcasted_iota(jnp.int32, (group * slots, depth), 1)

    def gather(table, send_buf, pull_buf, s, q_sem):
        def one_group(g, _):
            keys = col[pl.ds(g * group, group)].reshape(group * slots, slots)
            wide = jnp.concatenate([keys] * chunk_blocks, axis=1)

            def one_chunk(k, _):
                hot = jnp.where(wide - k * depth == lanes, 1.0, 0.0).astype(jnp.bfloat16)
                part = table[pl.ds(k * chunk_blocks, chunk_blocks)].reshape(depth, feat)
                found = jnp.dot(hot, part, preferred_element_type=jnp.float32)

                @pl.when(k == 0)
                def _():
                    acc[...] = found

                @pl.when(k > 0)
                def _():
                    acc[...] += found

                return 0

            lax.fori_loop(0, home_blocks // chunk_blocks, one_chunk, 0)
            send_buf[pl.ds(g * group, group)] = (
                acc[...].astype(jnp.bfloat16).reshape(group, slots, feat)
            )

            def send_one(i, _):
                j = g * group + i

                @pl.when(j < D - 1)
                def _():
                    q = lax.rem(d + D - offset(j), D)
                    pltpu.make_async_remote_copy(
                        src_ref=send_buf.at[j], dst_ref=pull_buf.at[d], send_sem=s, recv_sem=q_sem,
                        device_id=(q, r), device_id_type=MESH,
                    ).start()

                return 0

            lax.fori_loop(0, group, send_one, 0)
            return 0

        lax.fori_loop(0, D // group, one_group, 0)
        pull_buf[d] = send_buf[D - 1]

    copies[0].wait()
    gather(hist_av, send_a, pull_a, a_s, a_r)
    copies[3].wait()
    gather(hist_bv, send_b, pull_b, b_s, b_r)
    for i in (1, 2, 4, 5, 6, 7):
        copies[i].wait()

    def product(i, picks):
        left = jnp.concatenate([vals_v[i, t] for t, _ in picks], axis=1)
        right = jnp.concatenate([b for _, b in picks], axis=0)
        return jnp.dot(left, right, preferred_element_type=jnp.float32)

    far_base = blocks + home_blocks

    def near(i, _):
        picks = [(0, cur_v[cols[i, 0]])]
        picks += [(t, hist_av[jnp.maximum(cols[i, t] - blocks, 0)]) for t in range(1, home)]
        acc_a[i] = product(i, picks)
        acc_b[i] = product(i, [(t, hist_bv[jnp.maximum(cols[i, t] - blocks, 0)]) for t in range(1, home)])
        return 0

    lax.fori_loop(0, blocks, near, 0)

    def finish(i, acc_ref, pull_buf, w, number, factor_weight):
        far = product(i, [(t, pull_buf[jnp.maximum(cols[i, t] - far_base, 0)]) for t in range(home, tiles)])
        summed = acc_ref[i] + far
        mixed = (1.0 - restart) * summed + restart * zero_v[i].astype(jnp.float32)
        low = mixed.astype(jnp.bfloat16)
        prod = jnp.dot(low, w[...], preferred_element_type=jnp.float32)
        inner = (1.0 - factor_weight) * mixed + factor_weight * prod
        return jnp.maximum(inner, 0.0).astype(jnp.bfloat16), low

    whole(pull_a, D - 1, a_s, a_r).wait_recv()
    factor_two = math.log(strength / 2 + 1.0)
    factor_three = math.log(strength / 3 + 1.0)

    def second(i, _):
        rows = finish(i, acc_a, pull_a, w2_v, 2, factor_two)[0]
        fresh_v[i] = rows
        hist_out[r, i] = rows
        return 0

    lax.fori_loop(0, blocks, second, 0)

    def fresh_copy(src, slot, target, k):
        return pltpu.make_async_remote_copy(
            src_ref=src, dst_ref=hist_out.at[slot], send_sem=f_s.at[k], recv_sem=f_r.at[k],
            device_id=(d, target), device_id_type=MESH,
        )

    fresh = hist_out.at[r]
    side = lax.rem(r, 2)
    mate = r + 1 - 2 * side
    if R == 4:
        across = lax.rem(r + 2, R)
        sends = [fresh_copy(fresh, r, across, 0), fresh_copy(fresh, r, mate, 1)]
        forward = fresh_copy(hist_out.at[across], across, mate, 2)
    else:
        sends = [fresh_copy(fresh, r, lax.rem(r + 1 + k, R), k) for k in range(R - 1)]
        forward = None
    for c in sends:
        c.start()

    def own_tile(i, _):
        acc_b[i] += product(i, [(0, fresh_v[cols[i, 0]])])
        return 0

    lax.fori_loop(0, blocks, own_tile, 0)
    whole(pull_b, D - 1, b_s, b_r).wait_recv()

    def third(i, _):
        out, low = finish(i, acc_b, pull_b, w3_v, 3, factor_three)
        layer_out[i] = out
        low_v[i] = low
        return 0

    lax.fori_loop(0, blocks, third, 0)

    grad = factor_three * lax.dot_general(
        low_v[...].reshape(blocks * slots, feat), up_v[...].reshape(blocks * slots, feat),
        (((0,), (0,)), ((), ())), preferred_element_type=jnp.float32,
    )
    half = N // 2
    piece = g_send.shape[2]
    for c in range(N):
        g_send[c // half, c % half] = grad[c * piece:(c + 1) * piece, :]
    place = d * (R // 2) + lax.div(r, 2)
    to_mate = pltpu.make_async_remote_copy(
        src_ref=g_send.at[1 - side], dst_ref=g_mate, send_sem=m_s, recv_sem=m_r,
        device_id=(d, mate), device_id_type=MESH,
    )
    to_mate.start()
    to_mate.wait_recv()
    g_mate[...] += g_send[side]

    def scatter(k, _):
        t = lax.rem(place + 1 + k, half)
        pltpu.make_async_remote_copy(
            src_ref=g_mate.at[t], dst_ref=g_recv.at[place], send_sem=g_s, recv_sem=g_r,
            device_id=(lax.div(t, R // 2), 2 * lax.rem(t, R // 2) + side), device_id_type=MESH,
        ).start()
        return 0

    lax.fori_loop(0, half - 1, scatter, 0)
    g_recv[place] = g_mate[place]
    if forward is not None:
        sends[0].wait_recv()
        forward.start()
    whole(g_recv, half - 1, g_s, g_r).wait_recv()

    g_part[...] = jnp.sum(g_recv[...], axis=0).astype(g_part.dtype)
    mine = side * half + place

    def spread(k, _):
        t = lax.rem(me + 1 + k, N)
        pltpu.make_async_remote_copy(
            src_ref=g_part, dst_ref=g_all.at[mine], send_sem=p_s, recv_sem=p_r,
            device_id=(lax.div(t, R), lax.rem(t, R)), device_id_type=MESH,
        ).start()
        return 0

    lax.fori_loop(0, N - 1, spread, 0)
    g_all[mine] = g_part[...]
    whole(g_all, N - 1, p_s, p_r).wait_recv()
    grad_res[...] = g_all[...].astype(jnp.float32)

    if forward is not None:
        sends[1].wait_recv()
        forward.wait_recv()
        forward.wait_send()
    else:
        for c in sends:
            c.wait_recv()
    for c in sends:
        c.wait_send()
    whole(ask, D - 1, idx_s, idx_r).wait_send()
    whole(send_a, D - 1, a_s, a_r).wait_send()
    whole(send_b, D - 1, b_s, b_r).wait_send()
    to_mate.wait_send()
    whole(g_recv, half - 1, g_s, g_r).wait_send()
    whole(g_all, N - 1, p_s, p_r).wait_send()


def hand_over(parts, *refs):
    sources, targets, sem = refs[:3], refs[3:6], refs[6]
    outs = []
    for n, src, dst in zip(parts, sources, targets):
        rows = src.shape[0] // n
        for i in range(n):
            at = pl.ds(i * rows, rows)
            outs.append(pltpu.make_async_copy(src.at[at], dst.at[at], sem.at[len(outs)]))
    for c in outs:
        c.start()
    for c in outs:
        c.wait()


def local(D, R, h_zero, h_prev, hist_a, hist_b, tile_vals, tile_cols, pull_rows, pull_counts,
          weight_two, weight_three, grad_out):
    blocks, tiles, tile = tile_vals.shape[:3]
    feat = hist_a.shape[1]
    N = D * R
    hist_blocks = hist_a.shape[0] // tile
    piece = feat // N
    bf, f32 = jnp.bfloat16, jnp.float32
    own = (blocks, tile, feat)
    hist = (hist_blocks, tile, feat)
    slots = pull_rows.shape[2]
    pulled = (D, slots, feat)
    group = 2 if D % 2 == 0 else 1
    vm = pltpu.VMEM
    dma = pltpu.SemaphoreType.DMA
    any_spec = pl.BlockSpec(memory_space=pl.ANY)
    smem = pl.BlockSpec(memory_space=pltpu.SMEM)
    vspec = pl.BlockSpec(memory_space=pltpu.VMEM)
    grant = 20 * 2**20 + D * slots * (8 * feat + 4 * slots)
    out3, fresh, grad = pl.pallas_call(
        functools.partial(kernel, D, R),
        out_shape=(
            jax.ShapeDtypeStruct(own, bf),
            jax.ShapeDtypeStruct((R,) + own, bf),
            jax.ShapeDtypeStruct((N, piece, feat), f32),
        ),
        in_specs=[smem, smem, vspec] + [any_spec] * 8,
        out_specs=(vspec, vspec, vspec),
        scratch_shapes=[
            vm(own, bf), vm(own, bf), vm(hist, bf), vm(hist, bf), vm(tile_vals.shape, bf),
            vm((feat, feat), bf), vm((feat, feat), bf), vm(own, bf),
            vm((D, 1, slots), jnp.int32), vm((D, 1, slots), jnp.int32),
            vm((D, slots, slots), jnp.int32),
            vm(pulled, bf), vm(pulled, bf), vm(pulled, bf), vm(pulled, bf),
            vm((group * slots, feat), f32), vm(own, f32), vm(own, f32),
            vm(own, bf), vm(own, bf),
            vm((2, N // 2, piece, feat), f32), vm((N // 2, piece, feat), f32),
            vm((N // 2, piece, feat), f32),
            vm((piece, feat), bf), vm((N, piece, feat), bf),
            dma((8,)), dma, dma, dma, dma, dma, dma,
            dma((max(R - 1, 3),)), dma((max(R - 1, 3),)), dma, dma, dma, dma, dma, dma,
        ],
        compiler_params=pltpu.CompilerParams(
            collective_id=0, has_side_effects=True, vmem_limit_bytes=grant
        ),
    )(
        *[
            pltpu.with_memory_space_constraint(x, pltpu.HBM)
            for x in (
                tile_cols, pull_counts, pull_rows, h_zero.reshape(own), h_prev.reshape(own),
                hist_a.reshape(hist), hist_b.reshape(hist), tile_vals, weight_two, weight_three,
                grad_out.reshape(own),
            )
        ]
    )
    flat = (
        out3.reshape(h_zero.shape),
        fresh.reshape(R * h_zero.shape[0], feat),
        grad.reshape(feat, feat),
    )
    parts = (4, 8, 1)
    return pl.pallas_call(
        functools.partial(hand_over, parts),
        out_shape=tuple(jax.ShapeDtypeStruct(x.shape, x.dtype) for x in flat),
        in_specs=[vspec] * 3,
        out_specs=(any_spec,) * 3,
        scratch_shapes=[dma((sum(parts),))],
        compiler_params=pltpu.CompilerParams(vmem_limit_bytes=8 * 1024 * 1024),
    )(*flat)


def solution(mesh):
    both = ("dev", "rep")
    return jax.shard_map(
        functools.partial(local, mesh.shape["dev"], mesh.shape["rep"]),
        mesh=mesh,
        in_specs=(
            P(both, None), P(both, None), P("dev", None), P("dev", None),
            P(both, None, None, None), P(both, None), P(both, None, None), P(both, None),
            P(), P(), P(both, None),
        ),
        out_specs=(P(both, None), P("dev", None), P()),
        check_vma=False,
    )
```

profile of v0, /device:TPU:0, one launch (start us, length us, event | category | flops | bytes accessed | tf_op | source)
XLA Modules:
  0.0 55.9 jit_solution(7097255622310514920)
XLA Ops:
  0.6 53.5 %shard_map.130 = (bf16[8,128,256]{2,1,0:T(8,128)(2,1)S(1)}, bf16[4,8,128,256]{3,2,1,0:T(8,128)(2,1)S(1)}, f32[32,8,256]{2,1,0:T(8,128)S(1)}) custom-call(s32[8,12]{1,0:T(8,128)} %cols.1, s32[1,8]{1,0:T(1,128)} %counts.1, s32[1,8,128]{2,1,0:T(8,128)} %rows_in.1, bf16[8,128,256]{2,1,0:T(8,128)(2,1)} %bitcast.13, bf16[8,128,256]{2,1,0:T(8,128)(2,1)} %bitcast.14, ...), custom_call_target="tpu_custom_call" | custom-call | tf_op jit(solution)/shard_map/pallas_call | solution.py:320
  54.2 1.7 %shard_map.131 = (bf16[1024,256]{1,0:T(8,128)(2,1)}, bf16[4096,256]{1,0:T(8,128)(2,1)}, f32[256,256]{1,0:T(8,128)}) custom-call(bf16[1024,256]{1,0:T(8,128)(2,1)S(1)} %bitcast.9, bf16[4096,256]{1,0:T(8,128)(2,1)S(1)} %bitcast.8, f32[256,256]{1,0:T(8,128)S(1)} %bitcast.10), custom_call_target="tpu_custom_call" | custom-call | tf_op jit(solution)/shard_map/pallas_call | solution.py:362
where the time goes:
time: 56.1 us; the launch traced here: 55.9 us
  Pallas kernels  55.2 us (98%)
  between operations  0.64 us (1%)
    pallas_call x1, Pallas kernels, local(): pl.pallas_call(functools.partial(kernel, D, R), out_shape=(jax.ShapeDtype...  53.5 us
    pallas_call x1, Pallas kernels, local(): pl.pallas_call(functools.partial(hand_over, parts), out_shape=tuple((jax....  1.68 us

commit v1 on v0

v1 whole, which is shorter than its diff:
```python
import functools
import math

import jax
import jax.numpy as jnp
from jax import lax
from jax.experimental import pallas as pl
from jax.experimental.pallas import tpu as pltpu
from jax.sharding import PartitionSpec as P

restart = 0.1
strength = 0.5
MESH = pl.DeviceIdType.MESH
scope = jax.named_scope


def kernel(
    D, R,
    cols_h, counts_h, rows_h,
    h_zero, h_prev, hist_a, hist_b, tile_vals, w_two, w_three, grad_out,
    layer_out, hist_out, grad_res,
    cols, counts, rows_in,
    zero_v, cur_v, hist_av, hist_bv, vals_v, far_v, w2_v, w3_v, up_v,
    ask, asked, col, send_a, send_b, pull_a, pull_b, acc, acc_a, acc_b,
    fresh_v, low_v, g_send, g_mate, g_recv, g_part, g_all,
    local_sem, stage_sem, idx_s, idx_r, a_s, a_r, b_s, b_r, f_s, f_r, m_s, m_r, g_s, g_r, p_s, p_r,
):
    N = D * R
    X = 2 if D % 2 == 0 else 1
    Z = D // X
    H = Z // 2
    d = lax.axis_index("dev")
    r = lax.axis_index("rep")
    z, x = lax.div(d, X), lax.rem(d, X)
    me = d * R + r
    slots = rows_in.shape[2]
    feat = hist_av.shape[2]
    blocks = vals_v.shape[0]
    tiles = vals_v.shape[1]
    home = 4
    home_blocks = hist_av.shape[0]
    far_base = blocks + home_blocks
    dense = tiles - home == D

    barrier = pltpu.get_barrier_semaphore()
    if R == 4:
        side = lax.rem(r, 2)
        mates = [r + 1 - 2 * side, lax.rem(r + 2, R)]
    else:
        side = lax.rem(r, 2)
        mates = [lax.rem(r + 1 + k, R) for k in range(R - 1)]

    def signal_dev(sem):
        for step in (1, -1):
            t = z + step

            @pl.when(jnp.logical_and(t >= 0, t < Z))
            def _():
                pl.semaphore_signal(sem, inc=1, device_id=(t * X + x, r), device_id_type=MESH)

        if X == 2:
            pl.semaphore_signal(sem, inc=1, device_id=(z * X + 1 - x, r), device_id_type=MESH)

    def wait_dev(sem, more):
        inner = lax.div(z + Z - 1, Z) + lax.div(2 * Z - 2 - z, Z)
        pl.semaphore_wait(sem, inner + X - 1 + more)

    def signal_rep(sem):
        for t in mates:
            pl.semaphore_signal(sem, inc=1, device_id=(d, t), device_id_type=MESH)

    signal_dev(barrier)
    signal_rep(barrier)

    loads = [
        (rows_h, rows_in), (counts_h, counts), (hist_a, hist_av), (tile_vals, vals_v), (cols_h, cols),
        (hist_b, hist_bv), (h_prev, cur_v), (h_zero, zero_v), (w_two, w2_v), (w_three, w3_v), (grad_out, up_v),
    ]
    copies = [pltpu.make_async_copy(s, t, local_sem.at[i]) for i, (s, t) in enumerate(loads)]
    for c in copies:
        c.start()
    copies[0].wait()
    copies[1].wait()

    lane = lax.broadcasted_iota(jnp.int32, (1, slots), 1)

    def mask_rows(p, _):
        ask[p] = jnp.where(lane < counts[0, p], rows_in[0, pl.ds(p, 1), :], -1)
        return 0

    lax.fori_loop(0, D, mask_rows, 0)

    def ask_peer(p):
        pltpu.make_async_remote_copy(
            src_ref=ask.at[p], dst_ref=asked.at[d], send_sem=idx_s.at[p], recv_sem=idx_r.at[d],
            device_id=(p, r), device_id_type=MESH,
        ).start()

    def ask_at(s):
        for step in (1, -1):
            t = z + step * (s + 1)

            @pl.when(jnp.logical_and(t >= 0, t < Z))
            def _():
                ask_peer(t * X + x)

            if X == 2:
                u = z + step * s
                ok = jnp.logical_and(u >= 0, u < Z)
                ok = jnp.logical_and(ok, s + (1 + step) > 0)

                @pl.when(ok)
                def _():
                    ask_peer(u * X + 1 - x)

    rounds = Z - 1 + X - 1
    with scope("stages"):
        wait_dev(barrier, len(mates))
        signal_dev(stage_sem.at[0])
        ask_at(0)

        def stage(s, _):
            wait_dev(stage_sem.at[s - 1], 0)

            @pl.when(s < rounds - 1)
            def _():
                signal_dev(stage_sem.at[s])

            ask_at(s)
            return 0

        for s in range(1, rounds) if rounds < 6 else ():
            stage(s, 0)
        if rounds >= 6:
            lax.fori_loop(1, rounds, stage, 0)
    signal_rep(stage_sem.at[rounds])
    asked[d] = ask[d]

    def plane(m):
        if Z % 2:
            return lax.rem(z + 1 + m, Z)
        up = lax.div(z, H)
        over = (1 - up) * (H + m) + up * (H - 1 - m)
        near = up * H + lax.rem(z - up * H + 1 + m, H)
        far = lax.div(m, H)
        return (1 - far) * over + far * near

    if dense:
        copies[3].wait()
        copies[4].wait()

        def spread_tiles(i, _):
            first = cols[i, home] - far_base
            for p in range(D):
                t = home + lax.rem(p - first + D, D)
                far_v[p // X, pl.ds(i * slots, slots), (p % X) * slots:(p % X + 1) * slots] = vals_v[i, t]
            return 0

        with scope("tiles"):
            lax.fori_loop(0, blocks, spread_tiles, 0)

    group = X
    chunk_blocks = 8
    depth = chunk_blocks * slots
    lanes = lax.broadcasted_iota(jnp.int32, (group * slots, depth), 1)

    def idx_copy(q):
        return pltpu.make_async_remote_copy(
            src_ref=ask.at[q], dst_ref=asked.at[q], send_sem=idx_s.at[q], recv_sem=idx_r.at[q],
            device_id=(q, r), device_id_type=MESH,
        )

    def gather(table, send_buf, pull_buf, s, q_sem, fresh_keys):
        def one_group(m, _):
            base = plane(m) * X
            if fresh_keys:
                for e in range(X):
                    q = base + e

                    @pl.when(q != d)
                    def _():
                        idx_copy(q).wait_recv()

                    col[q] = jnp.broadcast_to(asked[q], (slots, slots)).T
            keys = col[pl.ds(base, group)].reshape(group * slots, slots)
            wide = jnp.concatenate([keys] * chunk_blocks, axis=1)

            def one_chunk(k, _):
                hot = jnp.where(wide - k * depth == lanes, 1.0, 0.0).astype(jnp.bfloat16)
                part = table[pl.ds(k * chunk_blocks, chunk_blocks)].reshape(depth, feat)
                found = jnp.dot(hot, part, preferred_element_type=jnp.float32)

                @pl.when(k == 0)
                def _():
                    acc[...] = found

                @pl.when(k > 0)
                def _():
                    acc[...] += found

                return 0

            lax.fori_loop(0, home_blocks // chunk_blocks, one_chunk, 0)
            send_buf[pl.ds(base, group)] = (
                acc[...].astype(jnp.bfloat16).reshape(group, slots, feat)
            )
            for e in range(X):
                q = base + e

                @pl.when(q != d)
                def _():
                    pltpu.make_async_remote_copy(
                        src_ref=send_buf.at[q], dst_ref=pull_buf.at[d], send_sem=s.at[q],
                        recv_sem=q_sem.at[d], device_id=(q, r), device_id_type=MESH,
                    ).start()

            return 0

        lax.fori_loop(0, Z, one_group, 0)
        pull_buf[d] = send_buf[d]

    def block_copy(send_buf, pull_buf, s, q_sem, p):
        return pltpu.make_async_remote_copy(
            src_ref=send_buf.at[p], dst_ref=pull_buf.at[p], send_sem=s.at[p], recv_sem=q_sem.at[p],
            device_id=(p, r), device_id_type=MESH,
        )

    copies[2].wait()
    with scope("gather_a"):
        gather(hist_av, send_a, pull_a, a_s, a_r, True)
    copies[5].wait()
    with scope("gather_b"):
        gather(hist_bv, send_b, pull_b, b_s, b_r, False)
    waited = (0, 1, 2, 3, 4, 5) if dense else (0, 1, 2, 5)
    for i in range(len(copies)):
        if i not in waited:
            copies[i].wait()

    def product(i, picks):
        left = jnp.concatenate([vals_v[i, t] for t, _ in picks], axis=1)
        right = jnp.concatenate([b for _, b in picks], axis=0)
        return jnp.dot(left, right, preferred_element_type=jnp.float32)

    def near_tiles(i, _):
        picks = [(0, cur_v[cols[i, 0]])]
        picks += [(t, hist_av[jnp.maximum(cols[i, t] - blocks, 0)]) for t in range(1, home)]
        acc_a[i] = product(i, picks)
        acc_b[i] = product(i, [(t, hist_bv[jnp.maximum(cols[i, t] - blocks, 0)]) for t in range(1, home)])
        return 0

    with scope("near"):
        lax.fori_loop(0, blocks, near_tiles, 0)

    pl.semaphore_wait(stage_sem.at[rounds], len(mates))
    if R == 4:
        signal_rep(stage_sem.at[rounds + 1])
        pl.semaphore_wait(stage_sem.at[rounds + 1], len(mates))

    rows = blocks * slots

    def pull_plane(n, acc_ref, send_buf, pull_buf, s, q_sem):
        m = lax.rem(n + Z - 1, Z) if Z % 2 else lax.rem(n + H + (Z - 1 - H), Z)
        if Z % 2 == 0:
            m = jnp.where(n == 0, Z - 1, jnp.where(n < H, H + n - 1, n - H))
        zt = plane(m)
        for e in range(X):
            q = zt * X + e

            @pl.when(q != d)
            def _():
                block_copy(send_buf, pull_buf, s, q_sem, q).wait_recv()

        part = jnp.dot(
            far_v[zt], pull_buf[pl.ds(zt * X, X)].reshape(X * slots, feat),
            preferred_element_type=jnp.float32,
        )
        acc_ref[...] += part.reshape(blocks, slots, feat)

    def pull_all(acc_ref, send_buf, pull_buf, s, q_sem):
        if dense:
            for n in range(Z):
                pull_plane(n, acc_ref, send_buf, pull_buf, s, q_sem)
            return

        def one(k, _):
            p = lax.rem(d + 1 + k, D)
            block_copy(send_buf, pull_buf, s, q_sem, p).wait_recv()
            return 0

        lax.fori_loop(0, D - 1, one, 0)

        def far(i, _):
            acc_ref[i] += product(
                i, [(t, pull_buf[jnp.maximum(cols[i, t] - far_base, 0)]) for t in range(home, tiles)]
            )
            return 0

        lax.fori_loop(0, blocks, far, 0)

    factor_two = math.log(strength / 2 + 1.0)
    factor_three = math.log(strength / 3 + 1.0)

    def mix(acc_ref, at):
        return (1.0 - restart) * acc_ref[at] + restart * zero_v[at].astype(jnp.float32)

    def activate(mixed, low, w, factor):
        shape = mixed.shape
        prod = jnp.dot(low.reshape(-1, feat), w[...], preferred_element_type=jnp.float32)
        inner = (1.0 - factor) * mixed + factor * prod.reshape(shape)
        return jnp.maximum(inner, 0.0).astype(jnp.bfloat16)

    with scope("pull_a"):
        pull_all(acc_a, send_a, pull_a, a_s, a_r)

    step = 2 if blocks % 2 == 0 else 1
    pieces = blocks // step

    def fresh_copy(slot, target, k, c):
        at = pl.ds(c * step, step)
        return pltpu.make_async_remote_copy(
            src_ref=hist_out.at[slot, at], dst_ref=hist_out.at[slot, at], send_sem=f_s.at[k, c],
            recv_sem=f_r.at[k, c], device_id=(d, target), device_id_type=MESH,
        )

    if R == 4:
        mate, across = mates
        targets = [across, mate]
    else:
        mate, across = r + 1 - 2 * side, None
        targets = mates

    def second(c, _):
        at = pl.ds(c * step, step)
        mixed = mix(acc_a, at)
        made = activate(mixed, mixed.astype(jnp.bfloat16), w2_v, factor_two)
        fresh_v[at] = made
        hist_out[r, at] = made
        return 0

    with scope("second"):
        lax.fori_loop(0, pieces, second, 0)

        def send_fresh(c, _):
            for k, t in enumerate(targets):
                fresh_copy(r, t, k, c).start()
            return 0

        lax.fori_loop(0, pieces, send_fresh, 0)

    def own_tile(i, _):
        acc_b[i] += product(i, [(0, fresh_v[cols[i, 0]])])
        return 0

    with scope("own"):
        lax.fori_loop(0, blocks, own_tile, 0)

    with scope("pull_b"):
        pull_all(acc_b, send_b, pull_b, b_s, b_r)

    with scope("grad"):
        low_v[...] = mix(acc_b, slice(None)).astype(jnp.bfloat16)
        grad = factor_three * lax.dot_general(
            low_v[...].reshape(rows, feat), up_v[...].reshape(rows, feat),
            (((0,), (0,)), ((), ())), preferred_element_type=jnp.float32,
        )
        half = N // 2
        piece = g_send.shape[2]
        for c in range(N):
            g_send[c // half, c % half] = grad[c * piece:(c + 1) * piece, :]
    place = d * (R // 2) + lax.div(r, 2)
    to_mate = pltpu.make_async_remote_copy(
        src_ref=g_send.at[1 - side], dst_ref=g_mate, send_sem=m_s, recv_sem=m_r,
        device_id=(d, mate), device_id_type=MESH,
    )
    to_mate.start()

    def third(c, _):
        at = pl.ds(c * step, step)
        layer_out[at] = activate(mix(acc_b, at), low_v[at], w3_v, factor_three)
        return 0

    with scope("third"):
        lax.fori_loop(0, pieces, third, 0)

    def whole(ref, n, s, q):
        part = ref.at[pl.ds(0, n)]
        return pltpu.make_async_remote_copy(
            src_ref=part, dst_ref=part, send_sem=s, recv_sem=q,
            device_id=(lax.rem(d + 1, D), r), device_id_type=MESH,
        )

    with scope("mate"):
        to_mate.wait_recv()
    g_mate[...] += g_send[side]

    def scatter(k, _):
        t = lax.rem(place + 1 + k, half)
        pltpu.make_async_remote_copy(
            src_ref=g_mate.at[t], dst_ref=g_recv.at[place], send_sem=g_s, recv_sem=g_r,
            device_id=(lax.div(t, R // 2), 2 * lax.rem(t, R // 2) + side), device_id_type=MESH,
        ).start()
        return 0

    lax.fori_loop(0, half - 1, scatter, 0)
    g_recv[place] = g_mate[place]
    with scope("scatter"):
        whole(g_recv, half - 1, g_s, g_r).wait_recv()

    g_part[...] = jnp.sum(g_recv[...], axis=0).astype(g_part.dtype)
    mine = side * half + place

    def spread(k, _):
        t = lax.rem(me + 1 + k, N)
        pltpu.make_async_remote_copy(
            src_ref=g_part, dst_ref=g_all.at[mine], send_sem=p_s, recv_sem=p_r,
            device_id=(lax.div(t, R), lax.rem(t, R)), device_id_type=MESH,
        ).start()
        return 0

    lax.fori_loop(0, N - 1, spread, 0)
    g_all[mine] = g_part[...]

    if R == 4:
        def forward(c, _):
            fresh_copy(across, across, 0, c).wait_recv()
            fresh_copy(across, mate, 2, c).start()
            return 0

        with scope("forward"):
            lax.fori_loop(0, pieces, forward, 0)
    with scope("spread"):
        whole(g_all, N - 1, p_s, p_r).wait_recv()
    grad_res[...] = g_all[...].astype(jnp.float32)

    def drain(c, _):
        if R == 4:
            fresh_copy(r, mate, 1, c).wait_recv()
            fresh_copy(r, mate, 2, c).wait_recv()
            for k in range(3):
                fresh_copy(r, mate, k, c).wait_send()
        else:
            for k in range(R - 1):
                fresh_copy(r, mate, k, c).wait()
        return 0

    with scope("drain"):
        lax.fori_loop(0, pieces, drain, 0)

        def sent(k, _):
            p = lax.rem(d + 1 + k, D)
            idx_copy(p).wait_send()
            block_copy(send_a, pull_a, a_s, a_r, p).wait_send()
            block_copy(send_b, pull_b, b_s, b_r, p).wait_send()
            return 0

        lax.fori_loop(0, D - 1, sent, 0)
        to_mate.wait_send()
        whole(g_recv, half - 1, g_s, g_r).wait_send()
        whole(g_all, N - 1, p_s, p_r).wait_send()


def hand_over(parts, *refs):
    sources, targets, sem = refs[:3], refs[3:6], refs[6]
    outs = []
    for n, src, dst in zip(parts, sources, targets):
        rows = src.shape[0] // n
        for i in range(n):
            at = pl.ds(i * rows, rows)
            outs.append(pltpu.make_async_copy(src.at[at], dst.at[at], sem.at[len(outs)]))
    for c in outs:
        c.start()
    for c in outs:
        c.wait()


def local(D, R, h_zero, h_prev, hist_a, hist_b, tile_vals, tile_cols, pull_rows, pull_counts,
          weight_two, weight_three, grad_out):
    blocks, tiles, tile = tile_vals.shape[:3]
    feat = hist_a.shape[1]
    N = D * R
    hist_blocks = hist_a.shape[0] // tile
    piece = feat // N
    bf, f32 = jnp.bfloat16, jnp.float32
    own = (blocks, tile, feat)
    hist = (hist_blocks, tile, feat)
    slots = pull_rows.shape[2]
    pulled = (D, slots, feat)
    X = 2 if D % 2 == 0 else 1
    Z = D // X
    dense = tiles - 4 == D
    far = (Z, blocks * tile, X * tile) if dense else (1, 16, 128)
    pieces = blocks // 2 if blocks % 2 == 0 else blocks
    links = max(R - 1, 3)
    vm = pltpu.VMEM
    dma = pltpu.SemaphoreType.DMA
    any_spec = pl.BlockSpec(memory_space=pl.ANY)
    vspec = pl.BlockSpec(memory_space=pltpu.VMEM)
    grant = 24 * 2**20 + D * slots * (8 * feat + 4 * slots)
    out3, fresh, grad = pl.pallas_call(
        functools.partial(kernel, D, R),
        out_shape=(
            jax.ShapeDtypeStruct(own, bf),
            jax.ShapeDtypeStruct((R,) + own, bf),
            jax.ShapeDtypeStruct((N, piece, feat), f32),
        ),
        in_specs=[any_spec] * 11,
        out_specs=(vspec, vspec, vspec),
        scratch_shapes=[
            pltpu.SMEM(tile_cols.shape, jnp.int32), pltpu.SMEM(pull_counts.shape, jnp.int32),
            vm(pull_rows.shape, jnp.int32),
            vm(own, bf), vm(own, bf), vm(hist, bf), vm(hist, bf), vm(tile_vals.shape, bf), vm(far, bf),
            vm((feat, feat), bf), vm((feat, feat), bf), vm(own, bf),
            vm((D, 1, slots), jnp.int32), vm((D, 1, slots), jnp.int32),
            vm((D, slots, slots), jnp.int32),
            vm(pulled, bf), vm(pulled, bf), vm(pulled, bf), vm(pulled, bf),
            vm((X * slots, feat), f32), vm(own, f32), vm(own, f32),
            vm(own, bf), vm(own, bf),
            vm((2, N // 2, piece, feat), f32), vm((N // 2, piece, feat), f32),
            vm((N // 2, piece, feat), f32),
            vm((piece, feat), bf), vm((N, piece, feat), bf),
            dma((11,)), pltpu.SemaphoreType.REGULAR((Z + X,)),
            dma((D,)), dma((D,)), dma((D,)), dma((D,)), dma((D,)), dma((D,)),
            dma((links, pieces)), dma((links, pieces)), dma, dma, dma, dma, dma, dma,
        ],
        compiler_params=pltpu.CompilerParams(
            collective_id=0, has_side_effects=True, vmem_limit_bytes=grant
        ),
    )(
        *[
            pltpu.with_memory_space_constraint(x, pltpu.HBM)
            for x in (
                tile_cols, pull_counts, pull_rows, h_zero.reshape(own), h_prev.reshape(own),
                hist_a.reshape(hist), hist_b.reshape(hist), tile_vals, weight_two, weight_three,
                grad_out.reshape(own),
            )
        ]
    )
    flat = (
        out3.reshape(h_zero.shape),
        fresh.reshape(R * h_zero.shape[0], feat),
        grad.reshape(feat, feat),
    )
    parts = (4, 8, 1)
    return pl.pallas_call(
        functools.partial(hand_over, parts),
        out_shape=tuple(jax.ShapeDtypeStruct(x.shape, x.dtype) for x in flat),
        in_specs=[vspec] * 3,
        out_specs=(any_spec,) * 3,
        scratch_shapes=[dma((sum(parts),))],
        compiler_params=pltpu.CompilerParams(vmem_limit_bytes=8 * 1024 * 1024),
    )(*flat)


def solution(mesh):
    both = ("dev", "rep")
    return jax.shard_map(
        functools.partial(local, mesh.shape["dev"], mesh.shape["rep"]),
        mesh=mesh,
        in_specs=(
            P(both, None), P(both, None), P("dev", None), P("dev", None),
            P(both, None, None, None), P(both, None), P(both, None, None), P(both, None),
            P(), P(), P(both, None),
        ),
        out_specs=(P(both, None), P("dev", None), P()),
        check_vma=False,
    )
```

time: 56.1 us -> 49.9 us (0.89)
  Pallas kernels: 55.2 us -> 49 us
    pallas_call x1, Pallas kernels: 53.5 us -> 47.3 us  [local(): pl.pallas_call(functools.partial(kernel, D, R), out_shape=(jax.ShapeDtype...]
where the time goes in v1:
time: 49.9 us; the launch traced here: 49.7 us
  Pallas kernels  49 us (98%)
  between operations  0.64 us (1%)
    pallas_call x1, Pallas kernels, local(): pl.pallas_call(functools.partial(kernel, D, R), out_shape=(jax.ShapeDtype...  47.3 us
    pallas_call x1, Pallas kernels, local(): pl.pallas_call(functools.partial(hand_over, parts), out_shape=tuple((jax....  1.68 us

profile of v1, /device:TPU:0, one launch (start us, length us, event | category | flops | bytes accessed | tf_op | source)
XLA Modules:
  0.0 49.7 jit_solution(1316744992413992597)
XLA Ops:
  0.6 47.3 %shard_map.130 = (bf16[8,128,256]{2,1,0:T(8,128)(2,1)S(1)}, bf16[4,8,128,256]{3,2,1,0:T(8,128)(2,1)S(1)}, f32[32,8,256]{2,1,0:T(8,128)S(1)}) custom-call(s32[8,12]{1,0:T(8,128)} %cols_h.1, s32[1,8]{1,0:T(1,128)} %counts_h.1, s32[1,8,128]{2,1,0:T(8,128)} %rows_h.1, bf16[8,128,256]{2,1,0:T(8,128)(2,1)} %bitcast.13, bf16[8,128,256]{2,1,0:T(8,128)(2,1)} %bitcast.14, ...), custom_call_target="tpu_custom_call" | custom-call | tf_op jit(solution)/shard_map/pallas_call | solution.py:499
  48.0 1.7 %shard_map.131 = (bf16[1024,256]{1,0:T(8,128)(2,1)}, bf16[4096,256]{1,0:T(8,128)(2,1)}, f32[256,256]{1,0:T(8,128)}) custom-call(bf16[1024,256]{1,0:T(8,128)(2,1)S(1)} %bitcast.9, bf16[4096,256]{1,0:T(8,128)(2,1)S(1)} %bitcast.8, f32[256,256]{1,0:T(8,128)S(1)} %bitcast.10), custom_call_target="tpu_custom_call" | custom-call | tf_op jit(solution)/shard_map/pallas_call | solution.py:544

commit v2 on v1

v2 whole, which is shorter than its diff:
```python
import functools
import math

import jax
import jax.numpy as jnp
from jax import lax
from jax.experimental import pallas as pl
from jax.experimental.pallas import tpu as pltpu
from jax.sharding import PartitionSpec as P

restart = 0.1
strength = 0.5
MESH = pl.DeviceIdType.MESH
scope = jax.named_scope


def kernel(
    D, R,
    cols_h, counts_h, rows_h,
    h_zero, h_prev, hist_a, hist_b, tile_vals, w_two, w_three, grad_out,
    layer_out, hist_out, grad_res,
    cols, counts, rows_in,
    zero_v, cur_v, hist_av, hist_bv, vals_v, far_v, w2_v, w3_v, up_v,
    ask, asked, hi, hot, send_a, send_b, pull_a, pull_b, acc_a, acc_b,
    fresh_v, low_v, g_send, g_recv, g_part, g_all,
    local_sem, stage_sem, idx_s, idx_r, a_s, a_r, b_s, b_r, f_s, f_r, g_s, g_r, p_s, p_r,
):
    N = D * R
    X = 2 if D % 2 == 0 else 1
    Z = D // X
    H = Z // 2
    d = lax.axis_index("dev")
    r = lax.axis_index("rep")
    z, x = lax.div(d, X), lax.rem(d, X)
    me = d * R + r
    slots = rows_in.shape[2]
    feat = hist_av.shape[2]
    blocks = vals_v.shape[0]
    tiles = vals_v.shape[1]
    home = 4
    home_blocks = hist_av.shape[0]
    far_base = blocks + home_blocks
    dense = tiles - home == D

    barrier = pltpu.get_barrier_semaphore()
    if R == 4:
        side = lax.rem(r, 2)
        mates = [r + 1 - 2 * side, lax.rem(r + 2, R)]
    else:
        side = lax.rem(r, 2)
        mates = [lax.rem(r + 1 + k, R) for k in range(R - 1)]

    def signal_dev(sem):
        for step in (1, -1):
            t = z + step

            @pl.when(jnp.logical_and(t >= 0, t < Z))
            def _():
                pl.semaphore_signal(sem, inc=1, device_id=(t * X + x, r), device_id_type=MESH)

        if X == 2:
            pl.semaphore_signal(sem, inc=1, device_id=(z * X + 1 - x, r), device_id_type=MESH)

    def wait_dev(sem, more):
        inner = lax.div(z + Z - 1, Z) + lax.div(2 * Z - 2 - z, Z)
        pl.semaphore_wait(sem, inner + X - 1 + more)

    def signal_rep(sem):
        for t in mates:
            pl.semaphore_signal(sem, inc=1, device_id=(d, t), device_id_type=MESH)

    signal_dev(barrier)
    signal_rep(barrier)

    loads = [
        (rows_h, rows_in), (counts_h, counts), (hist_a, hist_av), (tile_vals, vals_v), (cols_h, cols),
        (hist_b, hist_bv), (h_prev, cur_v), (h_zero, zero_v), (w_two, w2_v), (w_three, w3_v), (grad_out, up_v),
    ]
    copies = [pltpu.make_async_copy(s, t, local_sem.at[i]) for i, (s, t) in enumerate(loads)]
    for c in copies:
        c.start()

    def ask_peer(p):
        pltpu.make_async_remote_copy(
            src_ref=ask.at[p], dst_ref=asked.at[d], send_sem=idx_s, recv_sem=idx_r.at[d],
            device_id=(p, r), device_id_type=MESH,
        ).start()

    def ask_at(s):
        for step in (1, -1):
            t = z + step * (s + 1)

            @pl.when(jnp.logical_and(t >= 0, t < Z))
            def _():
                ask_peer(t * X + x)

            if X == 2:
                u = z + step * s
                ok = jnp.logical_and(u >= 0, u < Z)
                ok = jnp.logical_and(ok, s + (1 + step) > 0)

                @pl.when(ok)
                def _():
                    ask_peer(u * X + 1 - x)

    rounds = Z - 1 + X - 1
    lane = lax.broadcasted_iota(jnp.int32, (1, slots), 1)

    def mask_rows(p, _):
        ask[p] = jnp.where(lane < counts[0, p], rows_in[0, pl.ds(p, 1), :], -1)
        return 0

    def plane(m):
        if Z % 2:
            return lax.rem(z + 1 + m, Z)
        up = lax.div(z, H)
        over = (1 - up) * (H + m) + up * (H - 1 - m)
        near = up * H + lax.rem(z - up * H + 1 + m, H)
        far = lax.div(m, H)
        return (1 - far) * over + far * near

    span = X * slots
    bits = span.bit_length() - 1
    lanes = lax.broadcasted_iota(jnp.int32, (slots, slots), 1)
    low_width = span // slots

    def keys(q):
        @pl.when(q != d)
        def _():
            pltpu.make_async_remote_copy(
                src_ref=ask.at[q], dst_ref=asked.at[q], send_sem=idx_s, recv_sem=idx_r.at[q],
                device_id=(q, r), device_id_type=MESH,
            ).wait_recv()

        key = jnp.broadcast_to(asked[q], (slots, slots)).T
        hi[q] = lax.shift_right_arithmetic(key, bits).astype(jnp.float32).astype(jnp.bfloat16)
        rest = jnp.bitwise_and(key, span - 1)
        for w in range(low_width):
            hot[q, :, w * slots:(w + 1) * slots] = jnp.where(
                rest - w * slots == lanes, 1.0, 0.0
            ).astype(jnp.bfloat16)

    spans = home_blocks // low_width
    unit = 4

    def pick(table, base, count):
        tag = hi[pl.ds(base, count)].reshape(count * slots, slots)
        tag = jnp.concatenate([tag] * low_width, axis=1)
        low = hot[pl.ds(base, count)].reshape(count * slots, span)
        found = None
        for k in range(0, spans, unit):
            left = jnp.concatenate(
                [jnp.where(tag == jnp.bfloat16(k + u), low, jnp.bfloat16(0)) for u in range(unit)], axis=1
            )
            part = table[k * low_width:(k + unit) * low_width].reshape(unit * span, feat)
            got = jnp.dot(left, part, preferred_element_type=jnp.float32)
            found = got if found is None else found + got
        return found.astype(jnp.bfloat16).reshape(count, slots, feat)

    def serve(table, send_buf, pull_buf, s, q_sem, base, count):
        send_buf[pl.ds(base, count)] = pick(table, base, count)
        for e in range(count):
            q = base if count == 1 else base + lax.rem(x + 1 + e, count)

            @pl.when(q != d)
            def _():
                pltpu.make_async_remote_copy(
                    src_ref=send_buf.at[q], dst_ref=pull_buf.at[d], send_sem=s,
                    recv_sem=q_sem.at[z], device_id=(q, r), device_id_type=MESH,
                ).start()

    first = plane(0) * X

    def start_first():
        copies[2].wait()
        asked[d] = ask[d]
        q = first + x
        keys(q)
        serve(hist_av, send_a, pull_a, a_s, a_r, q, 1)

    beside = jnp.logical_or(z == H - 1, z == H)

    with scope("stages"):
        wait_dev(barrier, len(mates))
        signal_dev(stage_sem.at[0])
        copies[0].wait()
        copies[1].wait()
        if D <= 8:
            for p in range(D):
                mask_rows(p, 0)
        else:
            lax.fori_loop(0, D, mask_rows, 0)
        ask_at(0)

        def stage(s, _):
            wait_dev(stage_sem.at[s - 1], 0)

            @pl.when(s < rounds - 1)
            def _():
                signal_dev(stage_sem.at[s])

            ask_at(s)
            return 0

        for s in range(1, rounds) if rounds < 6 else ():
            if s == rounds - 1 and Z == 4:
                @pl.when(beside)
                def _():
                    start_first()
            stage(s, 0)
        if rounds >= 6:
            lax.fori_loop(1, rounds, stage, 0)
    signal_rep(stage_sem.at[rounds])

    def plane_copy(pull_buf, s, q_sem, zt, n):
        at = pull_buf.at[pl.ds(zt * X, n)]
        return pltpu.make_async_remote_copy(
            src_ref=at, dst_ref=at, send_sem=s, recv_sem=q_sem.at[zt],
            device_id=(lax.rem(d + 1, D), r), device_id_type=MESH,
        )

    def gather_a(m, _):
        base = plane(m) * X
        for e in range(X):
            keys(base + e)
        serve(hist_av, send_a, pull_a, a_s, a_r, base, X)
        return 0

    if Z == 4:
        turn = 2 * lax.rem(lax.div(z + 1, 2), 2)
    else:
        turn = 0

    def gather_b(m, _):
        k = lax.rem(m + turn, Z)
        if Z % 2 == 0:
            k = jnp.where(k < H, H - 1 - k, k)
        serve(hist_bv, send_b, pull_b, b_s, b_r, plane(k) * X, X)
        return 0

    with scope("gather_a"):
        if Z == 4 and rounds > 1:
            @pl.when(jnp.logical_not(beside))
            def _():
                start_first()
        else:
            start_first()
        for e in range(1, X):
            q = first + lax.rem(x + e, X)
            keys(q)
            serve(hist_av, send_a, pull_a, a_s, a_r, q, 1)
        lax.fori_loop(1, Z, gather_a, 0)
        pull_a[d] = send_a[d]

    pl.semaphore_wait(stage_sem.at[rounds], len(mates))
    if R == 4:
        signal_rep(stage_sem.at[rounds + 1])
    copies[5].wait()
    held = Z - H * lax.div(turn, H) if Z == 4 else Z
    with scope("gather_b"):
        lax.fori_loop(0, held, gather_b, 0)

    if dense:
        copies[3].wait()
        copies[4].wait()

        def spread_tiles(i, _):
            first = cols[i, home] - far_base
            for p in range(D):
                t = home + lax.rem(p - first + D, D)
                far_v[p // X, pl.ds(i * slots, slots), (p % X) * slots:(p % X + 1) * slots] = vals_v[i, t]
            return 0

        with scope("tiles"):
            lax.fori_loop(0, blocks, spread_tiles, 0)
    waited = (0, 1, 2, 3, 4, 5) if dense else (0, 1, 2, 5)
    for i in range(len(copies)):
        if i not in waited:
            copies[i].wait()

    def product(i, picks):
        left = jnp.concatenate([vals_v[i, t] for t, _ in picks], axis=1)
        right = jnp.concatenate([b for _, b in picks], axis=0)
        return jnp.dot(left, right, preferred_element_type=jnp.float32)

    def near_tiles(i, _):
        picks = [(0, cur_v[cols[i, 0]])]
        picks += [(t, hist_av[jnp.maximum(cols[i, t] - blocks, 0)]) for t in range(1, home)]
        acc_a[i] = product(i, picks)
        acc_b[i] = product(i, [(t, hist_bv[jnp.maximum(cols[i, t] - blocks, 0)]) for t in range(1, home)])
        return 0

    with scope("near"):
        lax.fori_loop(0, blocks, near_tiles, 0)
    with scope("gather_b2"):
        lax.fori_loop(held, Z, gather_b, 0)
        pull_b[d] = send_b[d]

    rows = blocks * slots

    def pull_plane(n, acc_ref, pull_buf, s, q_sem):
        if n == 0 or Z % 2:
            m = (n + Z - 1) % Z
        else:
            m = H + n - 1 if n < H else n - H
        zt = plane(m)
        if n == 0:
            if X > 1:
                plane_copy(pull_buf, s, q_sem, zt, X - 1).wait_recv()
        else:
            plane_copy(pull_buf, s, q_sem, zt, X).wait_recv()

        part = jnp.dot(
            far_v[zt], pull_buf[pl.ds(zt * X, X)].reshape(X * slots, feat),
            preferred_element_type=jnp.float32,
        )
        acc_ref[...] += part.reshape(blocks, slots, feat)

    def pull_all(acc_ref, pull_buf, s, q_sem):
        if dense:
            for n in range(Z):
                pull_plane(n, acc_ref, pull_buf, s, q_sem)
            return

        if X > 1:
            plane_copy(pull_buf, s, q_sem, z, X - 1).wait_recv()

        def one(k, _):
            plane_copy(pull_buf, s, q_sem, lax.rem(z + 1 + k, Z), X).wait_recv()
            return 0

        lax.fori_loop(0, Z - 1, one, 0)

        def far(i, _):
            acc_ref[i] += product(
                i, [(t, pull_buf[jnp.maximum(cols[i, t] - far_base, 0)]) for t in range(home, tiles)]
            )
            return 0

        lax.fori_loop(0, blocks, far, 0)

    factor_two = math.log(strength / 2 + 1.0)
    factor_three = math.log(strength / 3 + 1.0)

    def mix(acc_ref, at):
        return (1.0 - restart) * acc_ref[at] + restart * zero_v[at].astype(jnp.float32)

    def activate(mixed, low, w, factor):
        shape = mixed.shape
        prod = jnp.dot(low.reshape(-1, feat), w[...], preferred_element_type=jnp.float32)
        inner = (1.0 - factor) * mixed + factor * prod.reshape(shape)
        return jnp.maximum(inner, 0.0).astype(jnp.bfloat16)

    with scope("pull_a"):
        pull_all(acc_a, pull_a, a_s, a_r)

    step = 2 if blocks % 2 == 0 else 1
    pieces = blocks // step
    early = pieces - pieces // 4

    def fresh_copy(slot, target, k, c, n=1):
        at = pl.ds(c * step, n * step)
        recv = f_r.at[c] if k == 0 else f_r.at[pieces + k - 1]
        return pltpu.make_async_remote_copy(
            src_ref=hist_out.at[slot, at], dst_ref=hist_out.at[slot, at], send_sem=f_s.at[k],
            recv_sem=recv, device_id=(d, target), device_id_type=MESH,
        )

    if R == 4:
        mate, across = mates
        targets = [across, mate]
    else:
        mate, across = r + 1 - 2 * side, None
        targets = mates

    def second(c, _):
        at = pl.ds(c * step, step)
        mixed = mix(acc_a, at)
        made = activate(mixed, mixed.astype(jnp.bfloat16), w2_v, factor_two)
        fresh_v[at] = made
        hist_out[r, at] = made
        return 0

    with scope("second"):
        lax.fori_loop(0, pieces, second, 0)

        def send_fresh(c, _):
            for k, t in enumerate(targets):
                fresh_copy(r, t, k, c).start()
            return 0

        lax.fori_loop(0, early, send_fresh, 0)

    def own_tile(i, _):
        acc_b[i] += product(i, [(0, fresh_v[cols[i, 0]])])
        return 0

    with scope("own"):
        lax.fori_loop(0, blocks, own_tile, 0)

    with scope("pull_b"):
        pull_all(acc_b, pull_b, b_s, b_r)

    with scope("grad"):
        low_v[...] = mix(acc_b, slice(None)).astype(jnp.bfloat16)
        grad = factor_three * lax.dot_general(
            low_v[...].reshape(rows, feat), up_v[...].reshape(rows, feat),
            (((0,), (0,)), ((), ())), preferred_element_type=jnp.float32,
        )
        owners, piece = g_send.shape[:2]
        for c in range(owners):
            g_send[c] = grad[c * piece:(c + 1) * piece, :].astype(g_send.dtype)

    if R & (R - 1):
        def place(t):
            return lax.div(t, R), lax.rem(t, R)
    else:
        def place(t):
            return lax.shift_right_logical(t, R.bit_length() - 1), jnp.bitwise_and(t, R - 1)

    if owners < N:
        def reducer(o):
            return (H - 1) * X + lax.div(o, R // 2), 2 * lax.rem(o, R // 2) + 1

        own_part = (d - (H - 1) * X) * (R // 2) + lax.div(r, 2)
        reduces = jnp.logical_and(side == 1, jnp.logical_and(own_part >= 0, own_part < owners))
        turned = lax.div(owners, 2) * (1 - lax.div(z, H))
    else:
        reducer, own_part, reduces, turned = place, me, me >= 0, 0

    if R == 4:
        pl.semaphore_wait(stage_sem.at[rounds + 1], len(mates))

    def scatter(k, _):
        o = lax.rem(k + turned, owners)
        there = reducer(o)

        @pl.when(there[0] * R + there[1] != me)
        def _():
            pltpu.make_async_remote_copy(
                src_ref=g_send.at[o], dst_ref=g_recv.at[me], send_sem=g_s, recv_sem=g_r,
                device_id=there, device_id_type=MESH,
            ).start()

        return 0

    lax.fori_loop(0, owners, scatter, 0)
    lax.fori_loop(early, pieces, send_fresh, 0)

    def third(c, _):
        at = pl.ds(c * step, step)
        layer_out[at] = activate(mix(acc_b, at), low_v[at], w3_v, factor_three)
        return 0

    with scope("third"):
        lax.fori_loop(0, pieces, third, 0)

    def whole(ref, n, s, q):
        part = ref.at[pl.ds(0, n)]
        return pltpu.make_async_remote_copy(
            src_ref=part, dst_ref=part, send_sem=s, recv_sem=q,
            device_id=(lax.rem(d + 1, D), r), device_id_type=MESH,
        )

    @pl.when(reduces)
    def _():
        g_recv[me] = g_send[own_part]
        with scope("scatter"):
            whole(g_recv, N - 1, g_s, g_r).wait_recv()
        g_part[...] = jnp.sum(g_recv[...].astype(jnp.float32), axis=0).astype(g_part.dtype)

        def spread(k, _):
            t = k + jnp.where(k >= me, 1, 0)
            pltpu.make_async_remote_copy(
                src_ref=g_part, dst_ref=g_all.at[own_part], send_sem=p_s, recv_sem=p_r,
                device_id=place(t), device_id_type=MESH,
            ).start()
            return 0

        lax.fori_loop(0, N - 1, spread, 0)
        g_all[own_part] = g_part[...]

    if R == 4:
        def forward(c, _):
            fresh_copy(across, across, 0, c).wait_recv()
            fresh_copy(across, mate, 2, c).start()
            return 0

        with scope("forward"):
            lax.fori_loop(0, pieces, forward, 0)
    with scope("spread"):
        @pl.when(reduces)
        def _():
            whole(g_all, owners - 1, p_s, p_r).wait_recv()

        @pl.when(jnp.logical_not(reduces))
        def _():
            whole(g_all, owners, p_s, p_r).wait_recv()

    grad_res[...] = g_all[...].astype(jnp.float32)

    with scope("drain"):
        if R == 4:
            for k in (1, 2):
                fresh_copy(r, mate, k, 0, pieces).wait_recv()
        else:
            def landed(c, _):
                fresh_copy(r, mate, 0, c).wait_recv()
                return 0

            lax.fori_loop(0, pieces, landed, 0)
            for k in range(1, R - 1):
                fresh_copy(r, mate, k, 0, pieces).wait_recv()
        for k in range(3 if R == 4 else R - 1):
            fresh_copy(r, mate, k, 0, pieces).wait_send()
        whole(ask, D - 1, idx_s, p_r).wait_send()
        whole(send_a, D - 1, a_s, p_r).wait_send()
        whole(send_b, D - 1, b_s, p_r).wait_send()

        @pl.when(reduces)
        def _():
            whole(g_send, owners - 1, g_s, g_r).wait_send()
            whole(g_recv, N - 1, p_s, p_r).wait_send()

        @pl.when(jnp.logical_not(reduces))
        def _():
            whole(g_send, owners, g_s, g_r).wait_send()


def hand_over(parts, *refs):
    sources, targets, sem = refs[:3], refs[3:6], refs[6]
    outs = []
    for n, src, dst in zip(parts, sources, targets):
        rows = src.shape[0] // n
        for i in range(n):
            at = pl.ds(i * rows, rows)
            outs.append(pltpu.make_async_copy(src.at[at], dst.at[at], sem.at[len(outs)]))
    for c in outs:
        c.start()
    for c in outs:
        c.wait()


def local(D, R, h_zero, h_prev, hist_a, hist_b, tile_vals, tile_cols, pull_rows, pull_counts,
          weight_two, weight_three, grad_out):
    blocks, tiles, tile = tile_vals.shape[:3]
    feat = hist_a.shape[1]
    N = D * R
    hist_blocks = hist_a.shape[0] // tile
    bf, f32 = jnp.bfloat16, jnp.float32
    own = (blocks, tile, feat)
    hist = (hist_blocks, tile, feat)
    slots = pull_rows.shape[2]
    pulled = (D, slots, feat)
    X = 2 if D % 2 == 0 else 1
    Z = D // X
    dense = tiles - 4 == D
    owners = X * R if Z % 2 == 0 and R % 2 == 0 else N
    piece = feat // owners
    far = (Z, blocks * tile, X * tile) if dense else (1, 16, 128)
    pieces = blocks // 2 if blocks % 2 == 0 else blocks
    links = max(R - 1, 3)
    vm = pltpu.VMEM
    dma = pltpu.SemaphoreType.DMA
    any_spec = pl.BlockSpec(memory_space=pl.ANY)
    vspec = pl.BlockSpec(memory_space=pltpu.VMEM)
    grant = 24 * 2**20 + D * slots * (8 * feat + 8 * slots)
    out3, fresh, grad = pl.pallas_call(
        functools.partial(kernel, D, R),
        out_shape=(
            jax.ShapeDtypeStruct(own, bf),
            jax.ShapeDtypeStruct((R,) + own, bf),
            jax.ShapeDtypeStruct((owners, piece, feat), f32),
        ),
        in_specs=[any_spec] * 11,
        out_specs=(vspec, vspec, vspec),
        scratch_shapes=[
            pltpu.SMEM(tile_cols.shape, jnp.int32), pltpu.SMEM(pull_counts.shape, jnp.int32),
            vm(pull_rows.shape, jnp.int32),
            vm(own, bf), vm(own, bf), vm(hist, bf), vm(hist, bf), vm(tile_vals.shape, bf), vm(far, bf),
            vm((feat, feat), bf), vm((feat, feat), bf), vm(own, bf),
            vm((D, 1, slots), jnp.int32), vm((D, 1, slots), jnp.int32),
            vm((D, slots, slots), bf), vm((D, slots, X * slots), bf),
            vm(pulled, bf), vm(pulled, bf), vm(pulled, bf), vm(pulled, bf),
            vm(own, f32), vm(own, f32),
            vm(own, bf), vm(own, bf),
            vm((owners, piece, feat), bf), vm((N, piece, feat), bf),
            vm((piece, feat), bf), vm((owners, piece, feat), bf),
            dma((11,)), pltpu.SemaphoreType.REGULAR((Z + X,)),
            dma, dma((D,)), dma, dma((Z,)), dma, dma((Z,)),
            dma((links,)), dma((pieces + links - 1,)), dma, dma, dma, dma,
        ],
        compiler_params=pltpu.CompilerParams(
            collective_id=0, has_side_effects=True, vmem_limit_bytes=grant
        ),
    )(
        *[
            pltpu.with_memory_space_constraint(x, pltpu.HBM)
            for x in (
                tile_cols, pull_counts, pull_rows, h_zero.reshape(own), h_prev.reshape(own),
                hist_a.reshape(hist), hist_b.reshape(hist), tile_vals, weight_two, weight_three,
                grad_out.reshape(own),
            )
        ]
    )
    flat = (
        out3.reshape(h_zero.shape),
        fresh.reshape(R * h_zero.shape[0], feat),
        grad.reshape(feat, feat),
    )
    parts = (4, 8, 1)
    return pl.pallas_call(
        functools.partial(hand_over, parts),
        out_shape=tuple(jax.ShapeDtypeStruct(x.shape, x.dtype) for x in flat),
        in_specs=[vspec] * 3,
        out_specs=(any_spec,) * 3,
        scratch_shapes=[dma((sum(parts),))],
        compiler_params=pltpu.CompilerParams(vmem_limit_bytes=8 * 1024 * 1024),
    )(*flat)


def solution(mesh):
    both = ("dev", "rep")
    return jax.shard_map(
        functools.partial(local, mesh.shape["dev"], mesh.shape["rep"]),
        mesh=mesh,
        in_specs=(
            P(both, None), P(both, None), P("dev", None), P("dev", None),
            P(both, None, None, None), P(both, None), P(both, None, None), P(both, None),
            P(), P(), P(both, None),
        ),
        out_specs=(P(both, None), P("dev", None), P()),
        check_vma=False,
    )
```

time: 49.9 us -> 44.4 us (0.89)
  Pallas kernels: 49 us -> 43.6 us
    pallas_call x1, Pallas kernels: 47.3 us -> 41.9 us  [local(): pl.pallas_call(functools.partial(kernel, D, R), out_shape=(jax.ShapeDtype...]
where the time goes in v2:
time: 44.4 us; the launch traced here: 44.3 us
  Pallas kernels  43.6 us (98%)
  between operations  0.64 us (1%)
    pallas_call x1, Pallas kernels, local(): pl.pallas_call(functools.partial(kernel, D, R), out_shape=(jax.ShapeDtype...  41.9 us
    pallas_call x1, Pallas kernels, local(): pl.pallas_call(functools.partial(hand_over, parts), out_shape=tuple((jax....  1.68 us

profile of v2, /device:TPU:0, one launch (start us, length us, event | category | flops | bytes accessed | tf_op | source)
XLA Modules:
  0.0 44.3 jit_solution(2370133282941811824)
XLA Ops:
  0.6 41.9 %shard_map.130 = (bf16[8,128,256]{2,1,0:T(8,128)(2,1)S(1)}, bf16[4,8,128,256]{3,2,1,0:T(8,128)(2,1)S(1)}, f32[8,32,256]{2,1,0:T(8,128)S(1)}) custom-call(s32[8,12]{1,0:T(8,128)} %cols_h.1, s32[1,8]{1,0:T(1,128)} %counts_h.1, s32[1,8,128]{2,1,0:T(8,128)} %rows_h.1, bf16[8,128,256]{2,1,0:T(8,128)(2,1)} %bitcast.13, bf16[8,128,256]{2,1,0:T(8,128)(2,1)} %bitcast.14, ...), custom_call_target="tpu_custom_call" | custom-call | tf_op jit(solution)/shard_map/pallas_call | solution.py:568
  42.6 1.7 %shard_map.131 = (bf16[1024,256]{1,0:T(8,128)(2,1)}, bf16[4096,256]{1,0:T(8,128)(2,1)}, f32[256,256]{1,0:T(8,128)}) custom-call(bf16[1024,256]{1,0:T(8,128)(2,1)S(1)} %bitcast.9, bf16[4096,256]{1,0:T(8,128)(2,1)S(1)} %bitcast.8, f32[256,256]{1,0:T(8,128)S(1)} %bitcast.10), custom_call_target="tpu_custom_call" | custom-call | tf_op jit(solution)/shard_map/pallas_call | solution.py:612

commit v3 on v2

--- a/solution.py
+++ b/solution.py
@@ -22,8 +22,8 @@
     cols, counts, rows_in,
     zero_v, cur_v, hist_av, hist_bv, vals_v, far_v, w2_v, w3_v, up_v,
     ask, asked, hi, hot, send_a, send_b, pull_a, pull_b, acc_a, acc_b,
-    fresh_v, low_v, g_send, g_recv, g_part, g_all,
-    local_sem, stage_sem, idx_s, idx_r, a_s, a_r, b_s, b_r, f_s, f_r, g_s, g_r, p_s, p_r,
+    fresh_v, low_v, g_term, g_mate, g_send, g_recv, g_part, g_all,
+    local_sem, stage_sem, idx_s, idx_r, a_s, a_r, b_s, b_r, f_s, f_r, m_s, m_r, g_s, g_r, p_s, p_r,
 ):
     N = D * R
     X = 2 if D % 2 == 0 else 1
@@ -159,6 +159,9 @@
 
     def serve(table, send_buf, pull_buf, s, q_sem, base, count):
         send_buf[pl.ds(base, count)] = pick(table, base, count)
+        ship(send_buf, pull_buf, s, q_sem, base, count)
+
+    def ship(send_buf, pull_buf, s, q_sem, base, count):
         for e in range(count):
             q = base if count == 1 else base + lax.rem(x + 1 + e, count)
 
@@ -171,11 +174,13 @@
 
     first = plane(0) * X
 
-    def start_first():
-        copies[2].wait()
-        asked[d] = ask[d]
-        q = first + x
+    def start_block(e):
+        if e == 0:
+            asked[d] = ask[d]
+        q = first + lax.rem(x + e, X)
         keys(q)
+        if e == 0:
+            copies[2].wait()
         serve(hist_av, send_a, pull_a, a_s, a_r, q, 1)
 
     beside = jnp.logical_or(z == H - 1, z == H)
@@ -203,10 +208,10 @@
             return 0
 
         for s in range(1, rounds) if rounds < 6 else ():
-            if s == rounds - 1 and Z == 4:
+            if Z == 4 and s >= 2:
                 @pl.when(beside)
                 def _():
-                    start_first()
+                    start_block(s - 2)
             stage(s, 0)
         if rounds >= 6:
             lax.fori_loop(1, rounds, stage, 0)
@@ -231,24 +236,30 @@
     else:
         turn = 0
 
+    holds = beside if dense and Z == 4 else jnp.logical_and(side == 1, False)
+
     def gather_b(m, _):
         k = lax.rem(m + turn, Z)
         if Z % 2 == 0:
             k = jnp.where(k < H, H - 1 - k, k)
-        serve(hist_bv, send_b, pull_b, b_s, b_r, plane(k) * X, X)
+        base = plane(k) * X
+        send_b[pl.ds(base, X)] = pick(hist_bv, base, X)
+
+        @pl.when(jnp.logical_or(k >= H, jnp.logical_not(holds)))
+        def _():
+            ship(send_b, pull_b, b_s, b_r, base, X)
+
         return 0
 
     with scope("gather_a"):
-        if Z == 4 and rounds > 1:
+        if Z == 4 and X == 2:
             @pl.when(jnp.logical_not(beside))
             def _():
-                start_first()
+                for e in range(X):
+                    start_block(e)
         else:
-            start_first()
-        for e in range(1, X):
-            q = first + lax.rem(x + e, X)
-            keys(q)
-            serve(hist_av, send_a, pull_a, a_s, a_r, q, 1)
+            for e in range(X):
+                start_block(e)
         lax.fori_loop(1, Z, gather_a, 0)
         pull_a[d] = send_a[d]
 
@@ -354,6 +365,13 @@
     with scope("pull_a"):
         pull_all(acc_a, pull_a, a_s, a_r)
 
+    if dense and Z == 4:
+        @pl.when(holds)
+        def _():
+            for m in range(H):
+                ship(send_b, pull_b, b_s, b_r, plane(H - 1 - m) * X, X)
+
+
     step = 2 if blocks % 2 == 0 else 1
     pieces = blocks // step
     early = pieces - pieces // 4
@@ -408,8 +426,13 @@
             (((0,), (0,)), ((), ())), preferred_element_type=jnp.float32,
         )
         owners, piece = g_send.shape[:2]
-        for c in range(owners):
-            g_send[c] = grad[c * piece:(c + 1) * piece, :].astype(g_send.dtype)
+        g_term[...] = grad.reshape(owners, piece, feat)
+
+    pair = r + 1 - 2 * side
+    to_mate = pltpu.make_async_remote_copy(
+        src_ref=g_term, dst_ref=g_mate, send_sem=m_s, recv_sem=m_r,
+        device_id=(d, pair), device_id_type=MESH,
+    )
 
     if R & (R - 1):
         def place(t):
@@ -418,33 +441,36 @@
         def place(t):
             return lax.shift_right_logical(t, R.bit_length() - 1), jnp.bitwise_and(t, R - 1)
 
-    if owners < N:
-        def reducer(o):
-            return (H - 1) * X + lax.div(o, R // 2), 2 * lax.rem(o, R // 2) + 1
-
-        own_part = (d - (H - 1) * X) * (R // 2) + lax.div(r, 2)
-        reduces = jnp.logical_and(side == 1, jnp.logical_and(own_part >= 0, own_part < owners))
-        turned = lax.div(owners, 2) * (1 - lax.div(z, H))
-    else:
-        reducer, own_part, reduces, turned = place, me, me >= 0, 0
+    half = R // 2
+    own_part = (d - (H - 1) * X) * half + lax.div(r, 2)
+    reduces = jnp.logical_and(side == 1, jnp.logical_and(own_part >= 0, own_part < owners))
+    turned = lax.div(owners, 2) * (1 - lax.div(z, H))
+    voice = d * half + lax.div(r, 2)
 
     if R == 4:
         pl.semaphore_wait(stage_sem.at[rounds + 1], len(mates))
 
-    def scatter(k, _):
-        o = lax.rem(k + turned, owners)
-        there = reducer(o)
-
-        @pl.when(there[0] * R + there[1] != me)
-        def _():
+    @pl.when(side == 1)
+    def _():
+        to_mate.start()
+
+    @pl.when(side == 0)
+    def _():
+        with scope("mate"):
+            to_mate.wait_recv()
+        g_send[...] = (g_term[...] + g_mate[...]).astype(g_send.dtype)
+
+        def scatter(k, _):
+            o = lax.rem(k + turned, owners)
             pltpu.make_async_remote_copy(
-                src_ref=g_send.at[o], dst_ref=g_recv.at[me], send_sem=g_s, recv_sem=g_r,
-                device_id=there, device_id_type=MESH,
+                src_ref=g_send.at[o], dst_ref=g_recv.at[voice], send_sem=g_s, recv_sem=g_r,
+                device_id=((H - 1) * X + lax.div(o, half), 2 * lax.rem(o, half) + 1),
+                device_id_type=MESH,
             ).start()
-
-        return 0
-
-    lax.fori_loop(0, owners, scatter, 0)
+            return 0
+
+        lax.fori_loop(0, owners, scatter, 0)
+
     lax.fori_loop(early, pieces, send_fresh, 0)
 
     def third(c, _):
@@ -464,9 +490,8 @@
 
     @pl.when(reduces)
     def _():
-        g_recv[me] = g_send[own_part]
         with scope("scatter"):
-            whole(g_recv, N - 1, g_s, g_r).wait_recv()
+            whole(g_recv, N // 2, g_s, g_r).wait_recv()
         g_part[...] = jnp.sum(g_recv[...].astype(jnp.float32), axis=0).astype(g_part.dtype)
 
         def spread(k, _):
@@ -519,10 +544,20 @@
 
         @pl.when(reduces)
         def _():
-            whole(g_send, owners - 1, g_s, g_r).wait_send()
-            whole(g_recv, N - 1, p_s, p_r).wait_send()
-
-        @pl.when(jnp.logical_not(reduces))
+            def sent(k, _):
+                pltpu.make_async_remote_copy(
+                    src_ref=g_part, dst_ref=g_all.at[own_part], send_sem=p_s, recv_sem=p_r,
+                    device_id=(d, pair), device_id_type=MESH,
+                ).wait_send()
+                return 0
+
+            lax.fori_loop(0, N - 1, sent, 0)
+
+        @pl.when(side == 1)
+        def _():
+            to_mate.wait_send()
+
+        @pl.when(side == 0)
         def _():
             whole(g_send, owners, g_s, g_r).wait_send()
 
@@ -555,7 +590,7 @@
     X = 2 if D % 2 == 0 else 1
     Z = D // X
     dense = tiles - 4 == D
-    owners = X * R if Z % 2 == 0 and R % 2 == 0 else N
+    owners = X * R
     piece = feat // owners
     far = (Z, blocks * tile, X * tile) if dense else (1, 16, 128)
     pieces = blocks // 2 if blocks % 2 == 0 else blocks
@@ -584,11 +619,12 @@
             vm(pulled, bf), vm(pulled, bf), vm(pulled, bf), vm(pulled, bf),
             vm(own, f32), vm(own, f32),
             vm(own, bf), vm(own, bf),
-            vm((owners, piece, feat), bf), vm((N, piece, feat), bf),
+            vm((owners, piece, feat), f32), vm((owners, piece, feat), f32),
+            vm((owners, piece, feat), bf), vm((N // 2, piece, feat), bf),
             vm((piece, feat), bf), vm((owners, piece, feat), bf),
             dma((11,)), pltpu.SemaphoreType.REGULAR((Z + X,)),
             dma, dma((D,)), dma, dma((Z,)), dma, dma((Z,)),
-            dma((links,)), dma((pieces + links - 1,)), dma, dma, dma, dma,
+            dma((links,)), dma((pieces + links - 1,)), dma, dma, dma, dma, dma, dma,
         ],
         compiler_params=pltpu.CompilerParams(
             collective_id=0, has_side_effects=True, vmem_limit_bytes=grant

time: 44.4 us -> 43.4 us (0.977)
  Pallas kernels: 43.6 us -> 42.6 us
    pallas_call x1, Pallas kernels: 41.9 us -> 41 us  [local(): pl.pallas_call(functools.partial(kernel, D, R), out_shape=(jax.ShapeDtype...]
where the time goes in v3:
time: 43.4 us; the launch traced here: 43.3 us
  Pallas kernels  42.6 us (98%)
  between operations  0.64 us (1%)
    pallas_call x1, Pallas kernels, local(): pl.pallas_call(functools.partial(kernel, D, R), out_shape=(jax.ShapeDtype...  41 us
    pallas_call x1, Pallas kernels, local(): pl.pallas_call(functools.partial(hand_over, parts), out_shape=tuple((jax....  1.68 us

profile of v3, /device:TPU:0, one launch (start us, length us, event | category | flops | bytes accessed | tf_op | source)
XLA Modules:
  0.0 43.3 jit_solution(4200741141581216626)
XLA Ops:
  0.6 41.0 %shard_map.130 = (bf16[8,128,256]{2,1,0:T(8,128)(2,1)S(1)}, bf16[4,8,128,256]{3,2,1,0:T(8,128)(2,1)S(1)}, f32[8,32,256]{2,1,0:T(8,128)S(1)}) custom-call(s32[8,12]{1,0:T(8,128)} %cols_h.1, s32[1,8]{1,0:T(1,128)} %counts_h.1, s32[1,8,128]{2,1,0:T(8,128)} %rows_h.1, bf16[8,128,256]{2,1,0:T(8,128)(2,1)} %bitcast.13, bf16[8,128,256]{2,1,0:T(8,128)(2,1)} %bitcast.14, ...), custom_call_target="tpu_custom_call" | custom-call | tf_op jit(solution)/shard_map/pallas_call | solution.py:603
  41.6 1.7 %shard_map.131 = (bf16[1024,256]{1,0:T(8,128)(2,1)}, bf16[4096,256]{1,0:T(8,128)(2,1)}, f32[256,256]{1,0:T(8,128)}) custom-call(bf16[1024,256]{1,0:T(8,128)(2,1)S(1)} %bitcast.9, bf16[4096,256]{1,0:T(8,128)(2,1)S(1)} %bitcast.8, f32[256,256]{1,0:T(8,128)S(1)} %bitcast.10), custom_call_target="tpu_custom_call" | custom-call | tf_op jit(solution)/shard_map/pallas_call | solution.py:648

commit v4 on v3

--- a/solution.py
+++ b/solution.py
@@ -23,7 +23,7 @@
     zero_v, cur_v, hist_av, hist_bv, vals_v, far_v, w2_v, w3_v, up_v,
     ask, asked, hi, hot, send_a, send_b, pull_a, pull_b, acc_a, acc_b,
     fresh_v, low_v, g_term, g_mate, g_send, g_recv, g_part, g_all,
-    local_sem, stage_sem, idx_s, idx_r, a_s, a_r, b_s, b_r, f_s, f_r, m_s, m_r, g_s, g_r, p_s, p_r,
+    local_sem, stage_sem, idx_s, idx_r, a_s, a_r, b_s, b_r, f_s, f_r, g_s, g_r, p_s, p_r,
 ):
     N = D * R
     X = 2 if D % 2 == 0 else 1
@@ -76,7 +76,8 @@
         (rows_h, rows_in), (counts_h, counts), (hist_a, hist_av), (tile_vals, vals_v), (cols_h, cols),
         (hist_b, hist_bv), (h_prev, cur_v), (h_zero, zero_v), (w_two, w2_v), (w_three, w3_v), (grad_out, up_v),
     ]
-    copies = [pltpu.make_async_copy(s, t, local_sem.at[i]) for i, (s, t) in enumerate(loads)]
+    prompt = 6
+    copies = [pltpu.make_async_copy(s, t, local_sem.at[min(i, prompt)]) for i, (s, t) in enumerate(loads)]
     for c in copies:
         c.start()
 
@@ -215,7 +216,7 @@
             stage(s, 0)
         if rounds >= 6:
             lax.fori_loop(1, rounds, stage, 0)
-    signal_rep(stage_sem.at[rounds])
+    signal_rep(stage_sem.at[rounds - 1])
 
     def plane_copy(pull_buf, s, q_sem, zt, n):
         at = pull_buf.at[pl.ds(zt * X, n)]
@@ -263,9 +264,9 @@
         lax.fori_loop(1, Z, gather_a, 0)
         pull_a[d] = send_a[d]
 
-    pl.semaphore_wait(stage_sem.at[rounds], len(mates))
+    pl.semaphore_wait(stage_sem.at[rounds - 1], len(mates))
     if R == 4:
-        signal_rep(stage_sem.at[rounds + 1])
+        signal_rep(stage_sem.at[rounds])
     copies[5].wait()
     held = Z - H * lax.div(turn, H) if Z == 4 else Z
     with scope("gather_b"):
@@ -284,10 +285,12 @@
 
         with scope("tiles"):
             lax.fori_loop(0, blocks, spread_tiles, 0)
-    waited = (0, 1, 2, 3, 4, 5) if dense else (0, 1, 2, 5)
-    for i in range(len(copies)):
-        if i not in waited:
-            copies[i].wait()
+    if not dense:
+        copies[3].wait()
+        copies[4].wait()
+    late_bytes = sum(math.prod(t.shape) for _, t in loads[prompt:])
+    span_all = pl.ds(0, late_bytes // (slots * feat))
+    pltpu.make_async_copy(hist_a.at[span_all], hist_av.at[span_all], local_sem.at[prompt]).wait()
 
     def product(i, picks):
         left = jnp.concatenate([vals_v[i, t] for t, _ in picks], axis=1)
@@ -309,7 +312,7 @@
 
     rows = blocks * slots
 
-    def pull_plane(n, acc_ref, pull_buf, s, q_sem):
+    def arrive(n, pull_buf, s, q_sem):
         if n == 0 or Z % 2:
             m = (n + Z - 1) % Z
         else:
@@ -321,15 +324,19 @@
         else:
             plane_copy(pull_buf, s, q_sem, zt, X).wait_recv()
 
+        return zt
+
+    def pull_plane(n, acc_ref, pull_buf, s, q_sem):
+        zt = arrive(n, pull_buf, s, q_sem)
         part = jnp.dot(
             far_v[zt], pull_buf[pl.ds(zt * X, X)].reshape(X * slots, feat),
             preferred_element_type=jnp.float32,
         )
         acc_ref[...] += part.reshape(blocks, slots, feat)
 
-    def pull_all(acc_ref, pull_buf, s, q_sem):
+    def pull_all(acc_ref, pull_buf, s, q_sem, count=Z):
         if dense:
-            for n in range(Z):
+            for n in range(count):
                 pull_plane(n, acc_ref, pull_buf, s, q_sem)
             return
 
@@ -374,13 +381,13 @@
 
     step = 2 if blocks % 2 == 0 else 1
     pieces = blocks // step
-    early = pieces - pieces // 4
+    early = pieces
 
     def fresh_copy(slot, target, k, c, n=1):
         at = pl.ds(c * step, n * step)
         recv = f_r.at[c] if k == 0 else f_r.at[pieces + k - 1]
         return pltpu.make_async_remote_copy(
-            src_ref=hist_out.at[slot, at], dst_ref=hist_out.at[slot, at], send_sem=f_s.at[k],
+            src_ref=hist_out.at[slot, at], dst_ref=hist_out.at[slot, at], send_sem=f_s,
             recv_sem=recv, device_id=(d, target), device_id_type=MESH,
         )
 
@@ -417,12 +424,20 @@
         lax.fori_loop(0, blocks, own_tile, 0)
 
     with scope("pull_b"):
-        pull_all(acc_b, pull_b, b_s, b_r)
-
+        pull_all(acc_b, pull_b, b_s, b_r, Z - 1)
+        acc_b[...] = mix(acc_b, slice(None))
+        last = arrive(Z - 1, pull_b, b_s, b_r) if dense else None
     with scope("grad"):
-        low_v[...] = mix(acc_b, slice(None)).astype(jnp.bfloat16)
+        mixed = acc_b[...].reshape(rows, feat)
+        if dense:
+            late = pull_b[pl.ds(last * X, X)].reshape(X * slots, feat)
+            part = jnp.dot(far_v[last], late, preferred_element_type=jnp.float32)
+            mixed = mixed + (1.0 - restart) * part
+            acc_b[...] = mixed.reshape(blocks, slots, feat)
+        low = mixed.astype(jnp.bfloat16)
+        low_v[...] = low.reshape(blocks, slots, feat)
         grad = factor_three * lax.dot_general(
-            low_v[...].reshape(rows, feat), up_v[...].reshape(rows, feat),
+            low, up_v[...].reshape(rows, feat),
             (((0,), (0,)), ((), ())), preferred_element_type=jnp.float32,
         )
         owners, piece = g_send.shape[:2]
@@ -430,7 +445,7 @@
 
     pair = r + 1 - 2 * side
     to_mate = pltpu.make_async_remote_copy(
-        src_ref=g_term, dst_ref=g_mate, send_sem=m_s, recv_sem=m_r,
+        src_ref=g_term, dst_ref=g_mate, send_sem=g_s, recv_sem=g_r,
         device_id=(d, pair), device_id_type=MESH,
     )
 
@@ -448,7 +463,7 @@
     voice = d * half + lax.div(r, 2)
 
     if R == 4:
-        pl.semaphore_wait(stage_sem.at[rounds + 1], len(mates))
+        pl.semaphore_wait(stage_sem.at[rounds], len(mates))
 
     @pl.when(side == 1)
     def _():
@@ -475,7 +490,7 @@
 
     def third(c, _):
         at = pl.ds(c * step, step)
-        layer_out[at] = activate(mix(acc_b, at), low_v[at], w3_v, factor_three)
+        layer_out[at] = activate(acc_b[at], low_v[at], w3_v, factor_three)
         return 0
 
     with scope("third"):
@@ -536,8 +551,7 @@
             lax.fori_loop(0, pieces, landed, 0)
             for k in range(1, R - 1):
                 fresh_copy(r, mate, k, 0, pieces).wait_recv()
-        for k in range(3 if R == 4 else R - 1):
-            fresh_copy(r, mate, k, 0, pieces).wait_send()
+        whole(hist_out, R - 1, f_s, p_r).wait_send()
         whole(ask, D - 1, idx_s, p_r).wait_send()
         whole(send_a, D - 1, a_s, p_r).wait_send()
         whole(send_b, D - 1, b_s, p_r).wait_send()
@@ -622,9 +636,9 @@
             vm((owners, piece, feat), f32), vm((owners, piece, feat), f32),
             vm((owners, piece, feat), bf), vm((N // 2, piece, feat), bf),
             vm((piece, feat), bf), vm((owners, piece, feat), bf),
-            dma((11,)), pltpu.SemaphoreType.REGULAR((Z + X,)),
+            dma((7,)), pltpu.SemaphoreType.REGULAR((Z + X - 1,)),
             dma, dma((D,)), dma, dma((Z,)), dma, dma((Z,)),
-            dma((links,)), dma((pieces + links - 1,)), dma, dma, dma, dma, dma, dma,
+            dma, dma((pieces + links - 1,)), dma, dma, dma, dma,
         ],
         compiler_params=pltpu.CompilerParams(
             collective_id=0, has_side_effects=True, vmem_limit_bytes=grant
@@ -644,7 +658,7 @@
         fresh.reshape(R * h_zero.shape[0], feat),
         grad.reshape(feat, feat),
     )
-    parts = (4, 8, 1)
+    parts = (1, 1, 1)
     return pl.pallas_call(
         functools.partial(hand_over, parts),
         out_shape=tuple(jax.ShapeDtypeStruct(x.shape, x.dtype) for x in flat),

time: 43.4 us -> 43.3 us (level)
  no operation moved by 1% of the time
where the time goes in v4:
time: 43.3 us; the launch traced here: 43.1 us
  Pallas kernels  42.4 us (98%)
  between operations  0.64 us (1%)
    pallas_call x1, Pallas kernels, local(): pl.pallas_call(functools.partial(kernel, D, R), out_shape=(jax.ShapeDtype...  40.9 us
    pallas_call x1, Pallas kernels, local(): pl.pallas_call(functools.partial(hand_over, parts), out_shape=tuple((jax....  1.59 us

profile of v4, /device:TPU:0, one launch (start us, length us, event | category | flops | bytes accessed | tf_op | source)
XLA Modules:
  0.0 43.1 jit_solution(3860110638206025810)
XLA Ops:
  0.6 40.9 %shard_map.130 = (bf16[8,128,256]{2,1,0:T(8,128)(2,1)S(1)}, bf16[4,8,128,256]{3,2,1,0:T(8,128)(2,1)S(1)}, f32[8,32,256]{2,1,0:T(8,128)S(1)}) custom-call(s32[8,12]{1,0:T(8,128)} %cols_h.1, s32[1,8]{1,0:T(1,128)} %counts_h.1, s32[1,8,128]{2,1,0:T(8,128)} %rows_h.1, bf16[8,128,256]{2,1,0:T(8,128)(2,1)} %bitcast.13, bf16[8,128,256]{2,1,0:T(8,128)(2,1)} %bitcast.14, ...), custom_call_target="tpu_custom_call" | custom-call | tf_op jit(solution)/shard_map/pallas_call | solution.py:617
  41.5 1.6 %shard_map.131 = (bf16[1024,256]{1,0:T(8,128)(2,1)}, bf16[4096,256]{1,0:T(8,128)(2,1)}, f32[256,256]{1,0:T(8,128)}) custom-call(bf16[1024,256]{1,0:T(8,128)(2,1)S(1)} %bitcast.9, bf16[4096,256]{1,0:T(8,128)(2,1)S(1)} %bitcast.8, f32[256,256]{1,0:T(8,128)S(1)} %bitcast.10), custom_call_target="tpu_custom_call" | custom-call | tf_op jit(solution)/shard_map/pallas_call | solution.py:662

commit v5 on v4

--- a/solution.py
+++ b/solution.py
@@ -423,6 +423,9 @@
     with scope("own"):
         lax.fori_loop(0, blocks, own_tile, 0)
 
+    if R == 4:
+        pl.semaphore_wait(stage_sem.at[rounds], len(mates))
+
     with scope("pull_b"):
         pull_all(acc_b, pull_b, b_s, b_r, Z - 1)
         acc_b[...] = mix(acc_b, slice(None))
@@ -462,9 +465,6 @@
     turned = lax.div(owners, 2) * (1 - lax.div(z, H))
     voice = d * half + lax.div(r, 2)
 
-    if R == 4:
-        pl.semaphore_wait(stage_sem.at[rounds], len(mates))
-
     @pl.when(side == 1)
     def _():
         to_mate.start()
@@ -484,7 +484,8 @@
             ).start()
             return 0
 
-        lax.fori_loop(0, owners, scatter, 0)
+        for k in range(owners):
+            scatter(k, 0)
 
     lax.fori_loop(early, pieces, send_fresh, 0)
 
@@ -579,7 +580,8 @@
 def hand_over(parts, *refs):
     sources, targets, sem = refs[:3], refs[3:6], refs[6]
     outs = []
-    for n, src, dst in zip(parts, sources, targets):
+    order = (1, 0, 2)
+    for n, src, dst in [(parts[k], sources[k], targets[k]) for k in order]:
         rows = src.shape[0] // n
         for i in range(n):
             at = pl.ds(i * rows, rows)

time: 43.3 us -> 43.2 us (level)
  no operation moved by 1% of the time
where the time goes in v5:
time: 43.2 us; the launch traced here: 43.1 us
  Pallas kernels  42.4 us (98%)
  between operations  0.64 us (1%)
    pallas_call x1, Pallas kernels, local(): pl.pallas_call(functools.partial(kernel, D, R), out_shape=(jax.ShapeDtype...  40.8 us
    pallas_call x1, Pallas kernels, local(): pl.pallas_call(functools.partial(hand_over, parts), out_shape=tuple((jax....  1.59 us

profile of v5, /device:TPU:0, one launch (start us, length us, event | category | flops | bytes accessed | tf_op | source)
XLA Modules:
  0.0 43.1 jit_solution(6999594186184575021)
XLA Ops:
  0.6 40.8 %shard_map.130 = (bf16[8,128,256]{2,1,0:T(8,128)(2,1)S(1)}, bf16[4,8,128,256]{3,2,1,0:T(8,128)(2,1)S(1)}, f32[8,32,256]{2,1,0:T(8,128)S(1)}) custom-call(s32[8,12]{1,0:T(8,128)} %cols_h.1, s32[1,8]{1,0:T(1,128)} %counts_h.1, s32[1,8,128]{2,1,0:T(8,128)} %rows_h.1, bf16[8,128,256]{2,1,0:T(8,128)(2,1)} %bitcast.13, bf16[8,128,256]{2,1,0:T(8,128)(2,1)} %bitcast.14, ...), custom_call_target="tpu_custom_call" | custom-call | tf_op jit(solution)/shard_map/pallas_call | solution.py:619
  41.5 1.6 %shard_map.131 = (bf16[1024,256]{1,0:T(8,128)(2,1)}, bf16[4096,256]{1,0:T(8,128)(2,1)}, f32[256,256]{1,0:T(8,128)}) custom-call(bf16[1024,256]{1,0:T(8,128)(2,1)S(1)} %bitcast.9, bf16[4096,256]{1,0:T(8,128)(2,1)S(1)} %bitcast.8, f32[256,256]{1,0:T(8,128)S(1)} %bitcast.10), custom_call_target="tpu_custom_call" | custom-call | tf_op jit(solution)/shard_map/pallas_call | solution.py:664
